TPU v7x, 256 devices: a 8x8x2 block of a 8x8x16 slice. The times are simulated.
256 devices in a mesh: groups: 2 (over z), owners: 16 (over x, core), sub: 8 (over y).
Axes of the slice: x: 8, y: 8, z: 2, core: 2. Of those that a mesh axis runs over, the one named last changes fastest.
The devices are a block of a 8x8x16 slice.
Arguments:
- embeddings: bfloat16 [131072, 768], P(('groups', 'owners', 'sub')), parts along dimension 0, may hold values from -6 to 6, as said below
- class_table: bfloat16 [1000, 768], replicated, may hold values from -6 to 6
- nearest: int32 [131072], P(('groups', 'owners', 'sub')), parts along dimension 0, may hold values from 0 to 999
- keep_class: int32 [1000], replicated, may hold values 0 or 1
- destination: int32 [131072, 1], P(('groups', 'owners', 'sub')), parts along dimension 0, may hold values from 0 to 127; in each aligned block of 512 rows (0 to 511, 512 to 1023, ...) at most 6 rows name the same one
Outputs:
- received_rows: bfloat16 [196608, 768], P(('groups', 'owners', 'sub')), parts along dimension 0
- received_score: bfloat16 [196608], P(('groups', 'owners', 'sub')), parts along dimension 0
- received_position: int32 [196608], P(('groups', 'owners', 'sub')), parts along dimension 0
- shard_totals: int32 [256], P('groups'), parts along dimension 0
There are 2 independent parts, one for each index of `groups`. A program takes and returns all parts, laid end to end along the dimension named above; an argument that names none is the same for every part. Nothing has to cross between parts.
Inputs may be any that keep to these rules, and one draw needn't show every extreme that they name: `destination`: in the rows of one device no loader shard is named by more than 6 rows. Counts of rows per loader shard may be packed several to an int32 word wherever they travel; this is an exception to the 16-bit rule below. `embeddings`: some rows are entirely zero.
All inputs are finite; a program needn't handle non-finite values.
Results may differ from a plain program's by a relative error of at most 0.001.
Values may be sent and summed in bfloat16 or wider, within the bound.
A program may use at most 64 MiB of HBM per device.

v0:
```python
import math

import jax
import jax.numpy as jnp
from jax import lax
from jax.sharding import Mesh
from jax.sharding import PartitionSpec as P

OWNERS_SUB = ("owners_0", "owners_1", "sub")
GROUPS_OWNERS_SUB = ("groups", "owners_0", "owners_1", "sub")


def sent_together(arrays, axis, split_dim, concat_dim, along):
    columns = [a.reshape(*a.shape[:along], -1) for a in arrays]
    both = jnp.concatenate(columns, axis=along)
    result, at, finished = (
        lax.all_to_all(both, axis, split_axis=split_dim, concat_axis=concat_dim, tiled=True),
        0,
        [],
    )
    for a, column in zip(arrays, columns):
        slab = result[..., at : at + column.shape[along]]
        finished.append(slab.reshape(*slab.shape[:along], *a.shape[along:]))
        at += column.shape[along]
    return tuple(finished)


def laid_out(tiles, dim):
    tiles = jnp.moveaxis(tiles, 0, dim)
    shape = tiles.shape
    return tiles.reshape(*shape[:dim], shape[dim] * shape[dim + 1], *shape[dim + 2 :])


def stacked_from(value, axes, sequence):
    tiles = value
    for k in sequence:
        tiles = lax.all_gather(tiles, axes[k])
    done = sequence[::-1]
    back = [done.index(k) for k in range(len(axes))]
    tiles = tiles.transpose(*back, *range(len(axes), tiles.ndim))
    return tiles.reshape(-1, *value.shape)


def gathered_by_axis(value, axes, sequence, dim):
    return laid_out(stacked_from(value, axes, sequence), dim)


def margins(row_block, near_block, class_table, inverse_class, keep_class):
    products = lax.dot_general(
        row_block, class_table, (((1,), (1,)), ((), ())), preferred_element_type=jnp.float32
    )
    row_float = row_block.astype(jnp.float32)
    inverse_row = lax.rsqrt(jnp.sum(row_float * row_float, axis=1) + 1e-06)
    cosine = products * inverse_row[:, None] * inverse_class[None, :]
    class_ids = jnp.arange(class_table.shape[0], dtype=jnp.int32)
    class_match = near_block[:, None] == class_ids[None, :]
    given_cos = jnp.sum(jnp.where(class_match, cosine, 0.0), axis=1)
    others = jnp.max(jnp.where(class_match, -1e30, cosine), axis=1)
    kept_flag = jnp.sum(jnp.where(class_match, keep_class[None, :], 0), axis=1)
    return (20.0 * (given_cos - others), kept_flag)


def place_column(column, capacity):
    before = jnp.cumsum(column) - column
    offsets = jnp.arange(capacity, dtype=jnp.int32)
    placed = jnp.where(offsets[None, :] < column[:, None], before[:, None] + offsets[None, :], -1)
    return placed.reshape(column.shape[0] * capacity)


def on_device(embeddings, class_table, nearest, keep_class, destination):
    shard_count = lax.axis_size(OWNERS_SUB)
    local_rows = embeddings.shape[0]
    feature_width = embeddings.shape[1]
    capacity = 3 * local_rows // (2 * shard_count)
    class_float = class_table.astype(jnp.float32)
    inverse_class = lax.rsqrt(jnp.sum(class_float * class_float, axis=1) + 1e-06)
    block_rows = math.gcd(local_rows, 512)

    def one_block(inputs):
        return margins(inputs[0], inputs[1], class_table, inverse_class, keep_class)

    margin_value, kept_flag = lax.map(
        one_block,
        (
            embeddings.reshape(local_rows // block_rows, block_rows, feature_width),
            nearest.reshape(local_rows // block_rows, block_rows),
        ),
    )
    margin_value = margin_value.reshape(local_rows)
    kept_flag = kept_flag.reshape(local_rows)
    target = destination[:, 0]
    shard_ids = jnp.arange(shard_count, dtype=jnp.int32)
    onehot = ((target[:, None] == shard_ids[None, :]) & (kept_flag[:, None] == 1)).astype(jnp.int32)
    running = jnp.cumsum(onehot, axis=0) - onehot
    local_rank = jnp.sum(running * onehot, axis=1)
    counts = jnp.sum(onehot, axis=0)
    slot_index = jnp.where(kept_flag == 1, target * capacity + local_rank, shard_count * capacity)
    send_rows = (
        jnp.zeros((shard_count * capacity, feature_width), jnp.bfloat16)
        .at[slot_index]
        .set(embeddings, mode="drop")
    )
    send_score = (
        jnp.zeros((shard_count * capacity,), jnp.bfloat16)
        .at[slot_index]
        .set(margin_value.astype(jnp.bfloat16), mode="drop")
    )
    got_rows, got_score = sent_together(
        (
            send_rows.reshape(shard_count, capacity, feature_width),
            send_score.reshape(shard_count, capacity),
        ),
        OWNERS_SUB,
        0,
        0,
        2,
    )
    received_rows = got_rows.reshape(shard_count * capacity, feature_width)
    received_score = got_score.reshape(shard_count * capacity)
    all_counts = gathered_by_axis(counts[None, :], OWNERS_SUB, (0, 2, 1), 0)
    own_index = lax.axis_index(OWNERS_SUB)
    column = jnp.sum(jnp.where(shard_ids[None, :] == own_index, all_counts, 0), axis=1)
    received_position = place_column(column, capacity)
    shard_totals = jnp.sum(all_counts, axis=0)
    return (received_rows, received_score, received_position, shard_totals)


def solution(mesh):
    split = Mesh(
        mesh.devices.reshape(mesh.shape["groups"], 8, 2, mesh.shape["sub"]),
        ("groups", "owners_0", "owners_1", "sub"),
    )
    in_specs = (
        P(GROUPS_OWNERS_SUB, None),
        P(),
        P(GROUPS_OWNERS_SUB),
        P(),
        P(GROUPS_OWNERS_SUB, None),
    )
    out_specs = (
        P(GROUPS_OWNERS_SUB, None),
        P(GROUPS_OWNERS_SUB),
        P(GROUPS_OWNERS_SUB),
        P("groups"),
    )
    return jax.shard_map(
        on_device, mesh=split, in_specs=in_specs, out_specs=out_specs, check_vma=False
    )
```

profile of v0, /device:TPU:513, one launch (start us, length us, event | category | flops | bytes accessed | tf_op | source)
XLA Modules:
  0.0 127.5 jit_solution(17202897359766314484)
XLA Ops:
  0.6 1.0 select_reduce_fusion.2
  1.7 1.4 %multiply_reduce_fusion.1 = f32[512]{0:T(512)S(1)} fusion(bf16[512,768]{1,0:T(8,128)(2,1)} %param.5), kind=kLoop, calls=%fused_computation.9 | loop fusion | flops 1179136 | bytes 788480 | tf_op jit(solution)/shard_map/while/body/eval_jaxpr/reduce_sum | solution.py:53
  3.1 0.0 copy-start.1
  3.1 0.0 copy-start.3
  3.1 1.9 %multiply_reduce_fusion = f32[1000]{0:T(1024)S(1)} fusion(bf16[1000,768]{1,0:T(8,128)(2,1)} %param.6), kind=kLoop, calls=%fused_computation.2 | loop fusion | flops 2303000 | bytes 1540000 | tf_op jit(solution)/shard_map/reduce_sum | solution.py:76
  5.0 0.1 copy.17
  5.2 0.1 copy.16
  5.3 0.3 fusion.4
  5.7 0.3 convert_reduce_fusion
  6.1 1.2 select_reduce_fusion
  7.3 2.8 %scatter_custom_fusion = bf16[768,768]{1,0:T(8,128)(2,1)S(1)} fusion(s32[512]{0:T(512)S(1)} %bitcast.35, bf16[512,768]{1,0:T(8,128)(2,1)S(1)} %copy-done.1, bf16[]{:T(256)} %constant.21.clone.1), kind=kCustom, calls=%fused_computation.10 | custom fusion | bytes 1179650 | tf_op jit(solution)/shard_map/scatter | solution.py:101
  10.2 3.8 %scatter_custom_fusion.1 = bf16[768]{0:T(1024)(128)(2,1)S(1)} fusion(s32[512]{0:T(512)S(1)} %bitcast.36, bf16[512]{0:T(512)(128)(2,1)S(1)} %multiply_convert_fusion, bf16[]{:T(256)} %constant.21.clone.1), kind=kCustom, calls=%fused_computation.35 | custom fusion | bytes 1538 | tf_op jit(solution)/shard_map/scatter | solution.py:106
  13.9 0.3 reshape_reshape.9
  14.2 0.4 reshape.128
  14.7 1.6 %pad_maximum_fusion = bf16[128,6,769]{2,1,0:T(8,128)(2,1)} fusion(bf16[128,6,1]{2,1,0:T(8,128)(2,1)S(1)} %reshape_reshape.9, bf16[128,6,768]{2,1,0:T(8,128)(2,1)S(1)} %reshape.128), kind=kLoop, calls=%fused_computation.8 | loop fusion | flops 2362368 | bytes 2362368 | tf_op jit(solution)/shard_map/concatenate | solution.py:15
  16.3 27.8 %all-to-all-start = ((bf16[128,6,769]{2,1,0:T(8,128)(2,1)}), bf16[128,6,769]{2,1,0:T(8,128)(2,1)S(1)}, u32[]{:S(2)}, u32[]{:S(2)}) async-start(bf16[128,6,769]{2,1,0:T(8,128)(2,1)} %pad_maximum_fusion), calls=%async_computation | async-start | bytes 3670016 | tf_op jit(solution)/shard_map/all_to_all | solution.py:17
  44.1 48.6 %all-gather.3 = s32[8,1,128]{2,1,0:T(1,128)S(1)} all-gather(s32[1,1,128]{2,1,0:T(1,128)S(1)} %bitcast.34), channel_id=2, replica_groups=mesh['groups'=2,'owners_0'=8,'owners_1'=2,'sub'=8] {'owners_0'}, dimensions={0}, use_global_device_ids=true | all-gather | bytes 4608 | tf_op jit(solution)/shard_map/all_gather | solution.py:37
  92.7 18.9 %all-gather.1 = s32[64,1,128]{2,1,0:T(1,128)S(1)} all-gather(s32[8,1,128]{2,1,0:T(1,128)S(1)} %all-gather.3), channel_id=3, replica_groups=mesh['groups'=2,'owners_0'=8,'owners_1'=2,'sub'=8] {'sub'}, dimensions={0}, use_global_device_ids=true | all-gather | bytes 36864 | tf_op jit(solution)/shard_map/all_gather | solution.py:37
  111.6 11.2 %all-gather.2 = s32[16,8,1,128]{3,1,2,0:T(8,128)S(1)} all-gather(s32[8,8,1,128]{3,1,2,0:T(8,128)S(1)} %bitcast.28), channel_id=4, replica_groups=mesh['groups'=2,'owners_0'=8,'owners_1'=2,'sub'=8] {'owners_1'}, dimensions={0}, use_global_device_ids=true | all-gather | bytes 98304 | tf_op jit(solution)/shard_map/all_gather | solution.py:37
  122.8 0.5 reduce_sum.88
  123.4 0.3 select_reduce_fusion.3
  123.7 0.1 copy.21
  123.8 0.1 lt.27
  123.9 0.1 reshape.154
  124.0 0.2 reduce-window.20
  124.2 0.1 reduce.6
  124.3 0.1 add_select_fusion
  124.4 0.7 select_n.46
  125.1 0.1 slice.17
  125.2 1.2 reshape.129
  126.5 0.2 slice_reduce_fusion
  126.7 0.7 reshape_reshape.8
  (21 shorter events, 0.2 us)
Async XLA Ops:
  0.6 4.5 %copy-start.2 = (s32[512,1]{0,1:T(1,128)S(1)}, s32[512,1]{0,1:T(1,128)}, u32[]{:S(2)}) copy-start(s32[512,1]{0,1:T(1,128)} %param.9) | copy-start | bytes 6148
  3.1 3.0 %copy-start = (bf16[1000,768]{1,0:T(8,128)(2,1)S(1)}, bf16[1000,768]{1,0:T(8,128)(2,1)}, u32[]{:S(2)}) copy-start(bf16[1000,768]{1,0:T(8,128)(2,1)} %param.6) | copy-start | bytes 4608004
  3.1 3.0 %copy-start.1 = (bf16[512,768]{1,0:T(8,128)(2,1)S(1)}, bf16[512,768]{1,0:T(8,128)(2,1)}, u32[]{:S(2)}) copy-start(bf16[512,768]{1,0:T(8,128)(2,1)} %param.5) | copy-start | bytes 2359300
  3.1 3.0 %copy-start.3 = (s32[512]{0:T(512)S(1)}, s32[512]{0:T(512)}, u32[]{:S(2)}) copy-start(s32[512]{0:T(512)} %param.7) | copy-start | bytes 6148
  16.3 108.9 %all-to-all-start = ((bf16[128,6,769]{2,1,0:T(8,128)(2,1)}), bf16[128,6,769]{2,1,0:T(8,128)(2,1)S(1)}, u32[]{:S(2)}, u32[]{:S(2)}) async-start(bf16[128,6,769]{2,1,0:T(8,128)(2,1)} %pad_maximum_fusion), calls=%async_computation | async-start | bytes 3670016 | tf_op jit(solution)/shard_map/all_to_all | solution.py:17
where the time goes:
time: 128 us; the launch traced here: 127 us
  blocking collectives  78.8 us (62%)
  starting transfers between devices  27.8 us (22%)
  local copies, waits for them, and re-layouts  10.9 us (9%)
  other arithmetic  7.93 us (6%)
    all_gather x3, blocking collectives, stacked_from(): tiles = lax.all_gather(tiles, axes[k])  78.8 us
    all_to_all x1, starting transfers between devices, sent_together(): lax.all_to_all(both, axis, split_axis=split_dim, concat_axis=concat_dim,...  27.8 us
    scatter x1, local copies, waits for them, and re-layouts, on_device(): send_score = jnp.zeros((shard_count * capacity,), jnp.bfloat16).at[slot_i...  3.77 us
    scatter x1, local copies, waits for them, and re-layouts, on_device(): send_rows = jnp.zeros((shard_count * capacity, feature_width), jnp.bfloat...  2.83 us
  transfers between devices with their start and end apart: 1, of which 0 were waited for; matrix products, arithmetic and copies ran while one was open for 2% of the time, Pallas kernels for 0%

commit v1 on v0

v1 whole, which is shorter than its diff:
```python
import functools

import jax
import jax.numpy as jnp
from jax import lax
from jax.experimental import pallas as pl
from jax.experimental.pallas import tpu as pltpu
from jax.sharding import PartitionSpec as P

MESH = pl.DeviceIdType.MESH
BF = jnp.bfloat16
F32 = jnp.float32
ROWS_AXES = ("groups", "owners", "sub")


def iota(shape, dim):
    return lax.broadcasted_iota(jnp.int32, shape, dim)


def as_bf(mask):
    return jnp.where(mask, 1.0, 0.0).astype(BF)


def dot(a, b, dims):
    return lax.dot_general(a, b, (dims, ((), ())), preferred_element_type=F32)


def peer_of(step, own, sub, n_own, n_sub):
    shift = lax.rem(step * 37, n_own * n_sub)
    by_own, by_sub = shift // n_sub, lax.rem(shift, n_sub)
    chip = lax.rem(own // 2 + by_own // 2, n_own // 2)
    core = lax.rem(own + by_own, 2)
    return chip * 2 + core, lax.rem(sub + by_sub, n_sub)


def kernel(
    n_own, n_sub, cap,
    emb_hbm, table_hbm, near_hbm, keep_hbm, dest_hbm,
    rows_out, pos_out, score_out, total_out,
    emb, table, near, keep, dest, sbuf, smeta, rmeta,
    load_sem, own_sem, row_send, row_recv, meta_send, meta_recv,
):
    own, sub = lax.axis_index("owners"), lax.axis_index("sub")
    n = n_own * n_sub
    me = own * n_sub + sub
    rows, depth = emb.shape
    classes = table.shape[0]

    barrier = pltpu.get_barrier_semaphore()

    def greet(step, carry):
        o, s = peer_of(step, own, sub, n_own, n_sub)
        pl.semaphore_signal(
            barrier, inc=1, device_id={"owners": o, "sub": s}, device_id_type=MESH
        )
        return carry

    loads = [
        pltpu.make_async_copy(src, dst, load_sem.at[i])
        for i, (src, dst) in enumerate(
            (
                (near_hbm, near),
                (keep_hbm, keep),
                (dest_hbm, dest),
                (emb_hbm, emb),
                (table_hbm, table),
            )
        )
    ]
    for load in loads:
        load.start()
    lax.fori_loop(1, n, greet, 0)

    loads[0].wait()
    loads[1].wait()
    loads[2].wait()
    near_v = near[...]
    matches = near_v == iota((classes, rows), 0)
    kept = dot(keep[...].astype(F32).astype(BF), as_bf(matches), ((1,), (0,)))
    named = (dest[...] == iota((n, rows), 0)) & (kept > 0.5)
    named_bf = as_bf(named)
    earlier = as_bf(iota((rows, rows), 0) < iota((rows, rows), 1))
    running = dot(named_bf, earlier, ((1,), (0,)))
    rank = jnp.sum(jnp.where(named, running, 0.0), axis=0, keepdims=True).astype(jnp.int32)
    slot = jnp.where(kept > 0.5, dest[...] * cap + rank, -1)
    place = as_bf(slot == iota((n * cap, rows), 0))
    counts = dot(jnp.ones((8, rows), BF), named_bf, ((1,), (1,)))[:1]

    loads[3].wait()
    packed = dot(place, emb[...], ((1,), (0,))).astype(BF)
    sbuf[...] = packed.reshape(n, cap // 2, 2, depth)

    pl.semaphore_wait(barrier, n - 1)

    def send_rows(step, carry):
        o, s = peer_of(step, own, sub, n_own, n_sub)
        pltpu.make_async_remote_copy(
            sbuf.at[o * n_sub + s], rows_out.at[me], row_send, row_recv,
            device_id={"owners": o, "sub": s}, device_id_type=MESH,
        ).start()
        return carry

    lax.fori_loop(1, n, send_rows, 0)
    own_copy = pltpu.make_async_copy(sbuf.at[me], rows_out.at[me], own_sem)
    own_copy.start()

    loads[4].wait()
    emb_f = emb[...].astype(F32)
    row_square = jnp.sum(emb_f * emb_f, axis=1, keepdims=True)
    inv_row = lax.rsqrt(jnp.transpose(jnp.broadcast_to(row_square, (rows, 128)))[:1] + 1e-6)
    table_f = table[...].astype(F32)
    inv_class = lax.rsqrt(jnp.sum(table_f * table_f, axis=1, keepdims=True) + 1e-6)
    cosine = dot(table[...], emb[...], ((1,), (1,))) * inv_class
    given = jnp.sum(jnp.where(matches, cosine, 0.0), axis=0, keepdims=True)
    others = jnp.max(jnp.where(matches, -1e30, cosine), axis=0, keepdims=True)
    margin = (20.0 * ((given - others) * inv_row)).astype(BF).astype(F32)
    by_rank = jnp.where(rank == iota((8, rows), 0), margin, 0.0).astype(BF)
    scores = dot(named_bf, by_rank, ((1,), (1,)))
    scores = jnp.concatenate([scores, jnp.zeros((n, 120), F32)], axis=1)
    meta = jnp.stack([jnp.broadcast_to(counts, (n, n)), scores], axis=1)
    smeta[...] = meta.astype(BF)
    rmeta[me] = smeta[me]

    def send_meta(step, carry):
        o, s = peer_of(step, own, sub, n_own, n_sub)
        pltpu.make_async_remote_copy(
            smeta.at[o * n_sub + s], rmeta.at[me], meta_send, meta_recv,
            device_id={"owners": o, "sub": s}, device_id_type=MESH,
        ).start()
        return carry

    lax.fori_loop(1, n, send_meta, 0)
    part = pl.ds(0, n - 1)
    pltpu.make_async_copy(smeta.at[part], rmeta.at[part], meta_recv).wait()

    got = rmeta[...].astype(F32)
    got_counts, got_scores = got[:, 0, :], got[:, 1, :]
    slots = n * cap
    source = iota((n, slots), 1) // cap
    step_in = lax.rem(iota((1, slots), 1), cap)
    spread = as_bf(iota((n, slots), 0) == source)
    before = as_bf(iota((n, slots), 0) < source)
    counts_bf = got_counts.astype(BF)
    mine = iota((n, slots), 0) == me
    filled = jnp.sum(jnp.where(mine, dot(counts_bf, spread, ((0,), (0,))), 0.0), axis=0, keepdims=True)
    base = jnp.sum(jnp.where(mine, dot(counts_bf, before, ((0,), (0,))), 0.0), axis=0, keepdims=True)
    pos_out[...] = jnp.where(
        step_in < filled.astype(jnp.int32), base.astype(jnp.int32) + step_in, -1
    )
    spread_scores = dot(got_scores[:, :8].astype(BF), spread, ((0,), (0,)))
    score_out[...] = jnp.sum(
        jnp.where(iota((8, slots), 0) == step_in, spread_scores, 0.0), axis=0, keepdims=True
    ).astype(BF)
    total_out[...] = jnp.sum(got_counts, axis=0, keepdims=True).astype(jnp.int32)

    pltpu.make_async_copy(smeta.at[part], rmeta.at[part], meta_send).wait()
    pltpu.make_async_copy(sbuf.at[part], rows_out.at[part], row_send).wait()
    own_copy.wait()
    pltpu.make_async_copy(sbuf.at[part], rows_out.at[part], row_recv).wait()


def on_device(n_own, n_sub, embeddings, class_table, nearest, keep_class, destination):
    rows, depth = embeddings.shape
    classes = class_table.shape[0]
    n = n_own * n_sub
    cap = 3 * rows // (2 * n)
    slots = n * cap
    vmem = pl.BlockSpec(memory_space=pltpu.VMEM)
    hbm = pl.BlockSpec(memory_space=pl.ANY)
    got_rows, position, score, totals = pl.pallas_call(
        functools.partial(kernel, n_own, n_sub, cap),
        out_shape=(
            jax.ShapeDtypeStruct((n, cap // 2, 2, depth), BF),
            jax.ShapeDtypeStruct((1, slots), jnp.int32),
            jax.ShapeDtypeStruct((1, slots), BF),
            jax.ShapeDtypeStruct((1, n), jnp.int32),
        ),
        in_specs=[hbm] * 5,
        out_specs=(hbm, vmem, vmem, vmem),
        scratch_shapes=[
            pltpu.VMEM((rows, depth), BF),
            pltpu.VMEM((classes, depth), BF),
            pltpu.VMEM((1, rows), jnp.int32),
            pltpu.VMEM((1, classes), jnp.int32),
            pltpu.VMEM((1, rows), jnp.int32),
            pltpu.VMEM((n, cap // 2, 2, depth), BF),
            pltpu.VMEM((n, 2, 128), BF),
            pltpu.VMEM((n, 2, 128), BF),
            pltpu.SemaphoreType.DMA((5,)),
        ]
        + [pltpu.SemaphoreType.DMA] * 5,
        compiler_params=pltpu.CompilerParams(collective_id=0, has_side_effects=True),
    )(
        embeddings,
        class_table,
        nearest.reshape(1, rows),
        keep_class.reshape(1, classes),
        destination.reshape(1, rows),
    )
    return (
        got_rows.reshape(slots, depth),
        score.reshape(slots),
        position.reshape(slots),
        totals.reshape(n),
    )


def solution(mesh):
    spec = P(ROWS_AXES)
    return jax.shard_map(
        functools.partial(on_device, mesh.shape["owners"], mesh.shape["sub"]),
        mesh=mesh,
        in_specs=(P(ROWS_AXES, None), P(), spec, P(), P(ROWS_AXES, None)),
        out_specs=(P(ROWS_AXES, None), spec, spec, P("groups")),
        check_vma=False,
    )
```

time: 128 us -> 68.4 us (0.53)
  blocking collectives: 78.8 us -> 0 us
  Pallas kernels: 0 us -> 62.1 us
  starting transfers between devices: 27.8 us -> 0 us
  other arithmetic: 7.93 us -> 1.2 us
  local copies, waits for them, and re-layouts: 10.9 us -> 4.27 us
    all_gather x3 -> x0, blocking collectives: 78.8 us -> none  [stacked_from(): tiles = lax.all_gather(tiles, axes[k])]
    pallas_call x0 -> x1, Pallas kernels: none -> 62.1 us  [on_device(): pl.pallas_call(functools.partial(kernel, n_own, n_sub, cap), out_shape=(j...]
    all_to_all x1 -> x0, starting transfers between devices: 27.8 us -> none  [sent_together(): lax.all_to_all(both, axis, split_axis=split_dim, concat_axis=concat_dim,...]
    scatter x2 -> x0, local copies, waits for them, and re-layouts: 6.59 us -> none  [the longest x1 3.77 us: on_device(): send_score = jnp.zeros((shard_count * capacity,), jnp.bfloat16).at[slot_i...]
    reduce_sum x6 -> x0, other arithmetic: 5.49 us -> none  [the longest x1 1.91 us: on_device(): jnp.sum(class_float * class_float, axis=1) + 1e-06]
    reshape x2 -> x1, local copies, waits for them, and re-layouts: 1.67 us -> 3.74 us  [on_device(): got_rows.reshape(slots, depth)]
    concatenate x1 -> x0, other arithmetic: 1.61 us -> none  [sent_together(): both = jnp.concatenate(columns, axis=along)]
  transfers between devices with their start and end apart: 1 -> 0, of which waited for: 0 -> 0; matrix products, arithmetic and copies ran while one was open for 2% -> 0% of each run, Pallas kernels for 0% -> 0%
where the time goes in v1:
time: 68.4 us; the launch traced here: 68.3 us
  Pallas kernels  62.1 us (91%)
  local copies, waits for them, and re-layouts  4.27 us (6%)
  other arithmetic  1.2 us (2%)
    pallas_call x1, Pallas kernels, on_device(): pl.pallas_call(functools.partial(kernel, n_own, n_sub, cap), out_shape=(j...  62.1 us
    reshape x1, local copies, waits for them, and re-layouts, on_device(): got_rows.reshape(slots, depth)  3.74 us

profile of v1, /device:TPU:513, one launch (start us, length us, event | category | flops | bytes accessed | tf_op | source)
XLA Modules:
  0.0 68.3 jit_solution(13776024329342969131)
XLA Ops:
  0.6 62.1 %shard_map.84 = (bf16[128,3,2,768]{3,2,1,0:T(2,128)(2,1)}, s32[1,768]{1,0:T(1,128)}, bf16[1,768]{1,0:T(2,128)(2,1)}, s32[1,128]{1,0:T(1,128)}) custom-call(bf16[512,768]{1,0:T(8,128)(2,1)} %emb_hbm.1, bf16[1000,768]{1,0:T(8,128)(2,1)} %table_hbm.1, s32[1,512]{1,0:T(1,128)} %bitcast.5, s32[1,1000]{1,0:T(1,128)} %bitcast.4, s32[1,512]{1,0:T(1,128)} %bitcast.6), custom_call_target="tpu_custom_call" | custom-call | tf_op jit(solution)/shard_map/pallas_call | solution.py:170
  62.8 0.0 copy-start.1
  62.8 0.0 copy-start
  62.8 0.0 copy-start.2
  62.8 3.7 %reshape.32 = bf16[768,768]{1,0:T(8,128)(2,1)} reshape(bf16[128,3,2,768]{3,2,1,0:T(2,128)(2,1)} %get-tuple-element.8) | data formatting | bytes 2359296 | tf_op jit(solution)/shard_map/reshape | solution.py:201
  66.6 0.0 copy-done.1
  66.6 0.6 reduce
  67.2 0.0 copy-done
  67.2 0.6 reduce.1
  67.8 0.0 copy-done.2
  67.8 0.5 copy.10
Async XLA Ops:
  62.8 3.8 %copy-start.1 = (bf16[1,768]{1,0:T(2,128)(2,1)S(1)}, bf16[1,768]{1,0:T(2,128)(2,1)}, u32[]{:S(2)}) copy-start(bf16[1,768]{1,0:T(2,128)(2,1)} %get-tuple-element.9) | copy-start | bytes 4612
  62.8 4.4 %copy-start = (s32[1,768]{1,0:T(1,128)S(1)}, s32[1,768]{1,0:T(1,128)}, u32[]{:S(2)}) copy-start(s32[1,768]{1,0:T(1,128)} %get-tuple-element.10) | copy-start | bytes 9220
  62.8 5.0 %copy-start.2 = (s32[1,128]{1,0:T(1,128)S(1)}, s32[1,128]{1,0:T(1,128)}, u32[]{:S(2)}) copy-start(s32[1,128]{1,0:T(1,128)} %get-tuple-element.11) | copy-start | bytes 1540

commit v2 on v1

v2 whole, which is shorter than its diff:
```python
import functools

import jax
import jax.numpy as jnp
from jax import lax
from jax.experimental import pallas as pl
from jax.experimental.pallas import tpu as pltpu
from jax.sharding import PartitionSpec as P

MESH = pl.DeviceIdType.MESH
BF = jnp.bfloat16
F32 = jnp.float32
ROWS_AXES = ("groups", "owners", "sub")


def iota(shape, dim):
    return lax.broadcasted_iota(jnp.int32, shape, dim)


def as_bf(mask):
    return jnp.where(mask, 1.0, 0.0).astype(BF)


def dot(a, b, dims):
    return lax.dot_general(a, b, (dims, ((), ())), preferred_element_type=F32)


def turned(own, step, n_own):
    chip = lax.rem(own // 2 + step // 2, n_own // 2)
    return chip * 2 + lax.rem(own + step, 2)


def exchange(
    n_own, n_sub, cap,
    emb_hbm, table_hbm, near_hbm, keep_hbm, dest_hbm,
    got_rows, got_meta,
    emb, table, near, keep, dest, sbuf, smeta,
    load_sem, own_sem, row_send, row_recv, meta_send, meta_recv, in_sem, late_sem,
):
    own, sub = lax.axis_index("owners"), lax.axis_index("sub")
    n = n_own * n_sub
    me = own * n_sub + sub
    rows, depth = emb.shape
    classes = table.shape[0]

    barrier = pltpu.get_barrier_semaphore()
    late = me == 0
    early = jnp.logical_not(late)

    def tell(sem, o, s):
        pl.semaphore_signal(
            sem, inc=1, device_id={"owners": o, "sub": s}, device_id_type=MESH
        )

    loads = [
        pltpu.make_async_copy(src, dst, load_sem.at[i])
        for i, (src, dst) in enumerate(
            (
                (near_hbm, near),
                (keep_hbm, keep),
                (dest_hbm, dest),
                (emb_hbm, emb),
                (table_hbm, table),
            )
        )
    ]
    for load in loads:
        load.start()

    def greet_row(step, carry):
        o = turned(own, step, n_own)

        @pl.when(early & (o * n_sub + sub != 0))
        def _():
            tell(barrier, o, sub)

        return carry

    lax.fori_loop(1, n_own, greet_row, 0)

    loads[0].wait()
    loads[1].wait()
    loads[2].wait()
    near_v = near[...]
    matches = near_v == iota((classes, rows), 0)
    kept = dot(keep[...].astype(F32).astype(BF), as_bf(matches), ((1,), (0,)))
    named = (dest[...] == iota((n, rows), 0)) & (kept > 0.5)
    named_bf = as_bf(named)
    earlier = as_bf(iota((rows, rows), 0) < iota((rows, rows), 1))
    running = dot(named_bf, earlier, ((1,), (0,)))
    rank = jnp.sum(jnp.where(named, running, 0.0), axis=0, keepdims=True).astype(jnp.int32)
    slot = jnp.where(kept > 0.5, dest[...] * cap + rank, -1)
    place = as_bf(slot == iota((n * cap, rows), 0))
    counts = dot(jnp.ones((8, rows), BF), named_bf, ((1,), (1,)))[:1]

    loads[3].wait()
    packed = dot(place, emb[...], ((1,), (0,))).astype(BF)
    sbuf[...] = packed.reshape(n, cap // 2, 2, depth)

    @pl.when(early & (sub == 0))
    def _():
        pl.semaphore_wait(barrier, n_own - 2)
        tell(barrier, 0, 0)

    @pl.when(sub != 0)
    def _():
        pl.semaphore_wait(barrier, n_own - 1 + sub)

    @pl.when((own == 0) & (sub != 0))
    def _():
        tell(barrier, 0, 0)

    @pl.when(late)
    def _():
        pl.semaphore_wait(barrier, n_own - 1 + n_sub - 1)

    def tell_column(s, carry):
        @pl.when(early & (s > sub))
        def _():
            tell(barrier, own, s)

        @pl.when((own == 1) & (sub == 0) & (s > 0))
        def _():
            tell(barrier, 0, s)

        @pl.when((s < sub) & (own * n_sub + s != 0))
        def _():
            tell(in_sem.at[sub], own, s)

        return carry

    lax.fori_loop(0, n_sub, tell_column, 0)

    def tell_late(i, carry):
        @pl.when(late)
        def _():
            tell(late_sem, i // n_sub, lax.rem(i, n_sub))

        return carry

    lax.fori_loop(1, n, tell_late, 0)

    def send_rows(o, s):
        pltpu.make_async_remote_copy(
            sbuf.at[o * n_sub + s], got_rows.at[me], row_send, row_recv,
            device_id={"owners": o, "sub": s}, device_id_type=MESH,
        ).start()

    def send_meta(o, s):
        pltpu.make_async_remote_copy(
            smeta.at[o * n_sub + s], got_meta.at[me], meta_send, meta_recv,
            device_id={"owners": o, "sub": s}, device_id_type=MESH,
        ).start()

    def near_peers(act):
        def one(step, carry):
            shift = lax.rem(step * 37, n)
            o = turned(own, shift // n_sub, n_own)
            s = lax.rem(sub + shift, n_sub)

            @pl.when((late | (s <= sub)) & (o * n_sub + s != 0))
            def _():
                act(o, s)

            return carry

        lax.fori_loop(1, n, one, 0)

    near_peers(send_rows)
    own_rows = pltpu.make_async_copy(sbuf.at[me], got_rows.at[me], own_sem.at[0])
    own_rows.start()

    loads[4].wait()
    emb_f = emb[...].astype(F32)
    row_square = jnp.sum(emb_f * emb_f, axis=1, keepdims=True)
    inv_row = lax.rsqrt(jnp.transpose(jnp.broadcast_to(row_square, (rows, 128)))[:1] + 1e-6)
    table_f = table[...].astype(F32)
    inv_class = lax.rsqrt(jnp.sum(table_f * table_f, axis=1, keepdims=True) + 1e-6)
    cosine = dot(table[...], emb[...], ((1,), (1,))) * inv_class
    given = jnp.sum(jnp.where(matches, cosine, 0.0), axis=0, keepdims=True)
    rival = jnp.max(jnp.where(matches, -1e30, cosine), axis=0, keepdims=True)
    margin = (20.0 * ((given - rival) * inv_row)).astype(BF).astype(F32)
    by_rank = jnp.where(rank == iota((8, rows), 0), margin, 0.0).astype(BF)
    scores = dot(named_bf, by_rank, ((1,), (1,)))
    scores = jnp.concatenate([scores, jnp.zeros((n, 120), F32)], axis=1)
    meta = jnp.stack([jnp.broadcast_to(counts, (n, n)), scores], axis=1)
    smeta[...] = meta.astype(BF)

    near_peers(send_meta)
    own_meta = pltpu.make_async_copy(smeta.at[me], got_meta.at[me], own_sem.at[1])
    own_meta.start()

    for s in range(1, n_sub):

        @pl.when(early & (s > sub))
        def _():
            pl.semaphore_wait(in_sem.at[s], 1)

            def one(step, carry):
                o = turned(own, lax.rem(step * 5, n_own), n_own)
                send_rows(o, s)
                send_meta(o, s)
                return carry

            lax.fori_loop(0, n_own, one, 0)

    @pl.when(early)
    def _():
        pl.semaphore_wait(late_sem, 1)
        send_rows(0, 0)
        send_meta(0, 0)

    part = pl.ds(0, n - 1)
    pltpu.make_async_copy(sbuf.at[part], got_rows.at[part], row_send).wait()
    pltpu.make_async_copy(smeta.at[part], got_meta.at[part], meta_send).wait()
    own_rows.wait()
    own_meta.wait()
    pltpu.make_async_copy(sbuf.at[part], got_rows.at[part], row_recv).wait()
    pltpu.make_async_copy(smeta.at[part], got_meta.at[part], meta_recv).wait()


def finish(
    n_own, n_sub, cap,
    got_rows, got_meta,
    rows_out, score_out, pos_out, total_out,
    raw, meta, tidy, in_sem, out_sem, meta_sem,
):
    n = n_own * n_sub
    me = lax.axis_index("owners") * n_sub + lax.axis_index("sub")
    slots = n * cap
    depth = raw.shape[-1]
    load_meta = pltpu.make_async_copy(got_meta, meta, meta_sem)
    load_meta.start()
    loads, stores = [], []
    for g in range(n_own):
        block = pl.ds(g * n_sub, n_sub)
        span = pl.ds(g * n_sub * cap, n_sub * cap)
        loads.append(pltpu.make_async_copy(got_rows.at[block], raw.at[block], in_sem.at[g]))
        stores.append(pltpu.make_async_copy(tidy.at[span], rows_out.at[span], out_sem.at[g]))
        loads[-1].start()
    load_meta.wait()
    got = meta[...].astype(F32)
    got_counts, got_scores = got[:, 0, :], got[:, 1, :]
    source = iota((n, slots), 1) // cap
    step_in = lax.rem(iota((1, slots), 1), cap)
    spread = as_bf(iota((n, slots), 0) == source)
    before = as_bf(iota((n, slots), 0) < source)
    counts_bf = got_counts.astype(BF)
    mine = iota((n, slots), 0) == me
    filled = jnp.sum(
        jnp.where(mine, dot(counts_bf, spread, ((0,), (0,))), 0.0), axis=0, keepdims=True
    )
    base = jnp.sum(
        jnp.where(mine, dot(counts_bf, before, ((0,), (0,))), 0.0), axis=0, keepdims=True
    )
    pos_out[...] = jnp.where(
        step_in < filled.astype(jnp.int32), base.astype(jnp.int32) + step_in, -1
    ).reshape(slots)
    spread_scores = dot(got_scores[:, :8].astype(BF), spread, ((0,), (0,)))
    score_out[...] = (
        jnp.sum(
            jnp.where(iota((8, slots), 0) == step_in, spread_scores, 0.0), axis=0, keepdims=True
        )
        .astype(BF)
        .reshape(slots)
    )
    total_out[...] = jnp.sum(got_counts, axis=0, keepdims=True).astype(jnp.int32).reshape(n)
    for g in range(n_own):
        loads[g].wait()
        tidy[pl.ds(g * n_sub * cap, n_sub * cap), :] = raw[
            pl.ds(g * n_sub, n_sub)
        ].reshape(n_sub * cap, depth)
        stores[g].start()
    for store in stores:
        store.wait()


def on_device(n_own, n_sub, embeddings, class_table, nearest, keep_class, destination):
    rows, depth = embeddings.shape
    classes = class_table.shape[0]
    n = n_own * n_sub
    cap = 3 * rows // (2 * n)
    slots = n * cap
    vmem = pl.BlockSpec(memory_space=pltpu.VMEM)
    hbm = pl.BlockSpec(memory_space=pl.ANY)
    got_rows, got_meta = pl.pallas_call(
        functools.partial(exchange, n_own, n_sub, cap),
        out_shape=(
            jax.ShapeDtypeStruct((n, cap // 2, 2, depth), BF),
            jax.ShapeDtypeStruct((n, 2, 128), BF),
        ),
        in_specs=[hbm] * 5,
        out_specs=(hbm, hbm),
        scratch_shapes=[
            pltpu.VMEM((rows, depth), BF),
            pltpu.VMEM((classes, depth), BF),
            pltpu.VMEM((1, rows), jnp.int32),
            pltpu.VMEM((1, classes), jnp.int32),
            pltpu.VMEM((1, rows), jnp.int32),
            pltpu.VMEM((n, cap // 2, 2, depth), BF),
            pltpu.VMEM((n, 2, 128), BF),
            pltpu.SemaphoreType.DMA((5,)),
            pltpu.SemaphoreType.DMA((2,)),
            pltpu.SemaphoreType.DMA,
            pltpu.SemaphoreType.DMA,
            pltpu.SemaphoreType.DMA,
            pltpu.SemaphoreType.DMA,
            pltpu.SemaphoreType.REGULAR((n_sub,)),
            pltpu.SemaphoreType.REGULAR,
        ],
        compiler_params=pltpu.CompilerParams(collective_id=0, has_side_effects=True),
    )(
        embeddings,
        class_table,
        nearest.reshape(1, rows),
        keep_class.reshape(1, classes),
        destination.reshape(1, rows),
    )
    return pl.pallas_call(
        functools.partial(finish, n_own, n_sub, cap),
        out_shape=(
            jax.ShapeDtypeStruct((slots, depth), BF),
            jax.ShapeDtypeStruct((slots,), BF),
            jax.ShapeDtypeStruct((slots,), jnp.int32),
            jax.ShapeDtypeStruct((n,), jnp.int32),
        ),
        in_specs=[hbm, hbm],
        out_specs=(hbm, vmem, vmem, vmem),
        scratch_shapes=[
            pltpu.VMEM((n, cap // 2, 2, depth), BF),
            pltpu.VMEM((n, 2, 128), BF),
            pltpu.VMEM((slots, depth), BF),
            pltpu.SemaphoreType.DMA((n_own,)),
            pltpu.SemaphoreType.DMA((n_own,)),
            pltpu.SemaphoreType.DMA,
        ],
    )(got_rows, got_meta)


def solution(mesh):
    spec = P(ROWS_AXES)
    return jax.shard_map(
        functools.partial(on_device, mesh.shape["owners"], mesh.shape["sub"]),
        mesh=mesh,
        in_specs=(P(ROWS_AXES, None), P(), spec, P(), P(ROWS_AXES, None)),
        out_specs=(P(ROWS_AXES, None), spec, spec, P("groups")),
        check_vma=False,
    )
```

time: 68.4 us -> 72.5 us (1.060)
  the two profiles are of different devices: /device:TPU:513 before, /device:TPU:640 now
where the time goes in v2:
time: 72.5 us; the launch traced here: 72.4 us
  Pallas kernels  71.7 us (99%)
    pallas_call x1, Pallas kernels, on_device(): pl.pallas_call(functools.partial(exchange, n_own, n_sub, cap), out_shape=...  68.1 us
    pallas_call x1, Pallas kernels, on_device(): pl.pallas_call(functools.partial(finish, n_own, n_sub, cap), out_shape=(j...  3.65 us

profile of v2, /device:TPU:640, one launch (start us, length us, event | category | flops | bytes accessed | tf_op | source)
XLA Modules:
  0.0 72.4 jit_solution(18188296916299897313)
XLA Ops:
  0.6 68.1 %shard_map.84 = (bf16[128,3,2,768]{3,2,1,0:T(2,128)(2,1)}, bf16[128,2,128]{2,1,0:T(2,128)(2,1)}) custom-call(bf16[512,768]{1,0:T(8,128)(2,1)} %emb_hbm.1, bf16[1000,768]{1,0:T(8,128)(2,1)} %table_hbm.1, s32[1,512]{1,0:T(1,128)} %bitcast.4, s32[1,1000]{1,0:T(1,128)} %bitcast.3, s32[1,512]{1,0:T(1,128)} %bitcast.5), custom_call_target="tpu_custom_call" | custom-call | tf_op jit(solution)/shard_map/pallas_call | solution.py:286
  68.7 3.7 %shard_map.85 = (bf16[768,768]{1,0:T(8,128)(2,1)}, bf16[768]{0:T(1024)(128)(2,1)}, s32[768]{0:T(1024)}, s32[128]{0:T(128)}) custom-call(bf16[128,3,2,768]{3,2,1,0:T(2,128)(2,1)} %get-tuple-element.6.got_rows, bf16[128,2,128]{2,1,0:T(2,128)(2,1)} %get-tuple-element.7.got_meta), custom_call_target="tpu_custom_call" | custom-call | tf_op jit(solution)/shard_map/pallas_call | solution.py:319

commit v3 on v2

--- a/solution.py
+++ b/solution.py
@@ -45,6 +45,7 @@
 
     barrier = pltpu.get_barrier_semaphore()
     late = me == 0
+    hold = n * 5 // 8
     early = jnp.logical_not(late)
 
     def tell(sem, o, s):
@@ -152,21 +153,21 @@
             device_id={"owners": o, "sub": s}, device_id_type=MESH,
         ).start()
 
-    def near_peers(act):
+    def peers(act, first, last, which):
         def one(step, carry):
             shift = lax.rem(step * 37, n)
             o = turned(own, shift // n_sub, n_own)
             s = lax.rem(sub + shift, n_sub)
 
-            @pl.when((late | (s <= sub)) & (o * n_sub + s != 0))
+            @pl.when(which(s) & (o * n_sub + s != 0))
             def _():
                 act(o, s)
 
             return carry
 
-        lax.fori_loop(1, n, one, 0)
-
-    near_peers(send_rows)
+        lax.fori_loop(first, last, one, 0)
+
+    peers(send_rows, 1, hold, lambda s: late | (s <= sub))
     own_rows = pltpu.make_async_copy(sbuf.at[me], got_rows.at[me], own_sem.at[0])
     own_rows.start()
 
@@ -186,7 +187,6 @@
     meta = jnp.stack([jnp.broadcast_to(counts, (n, n)), scores], axis=1)
     smeta[...] = meta.astype(BF)
 
-    near_peers(send_meta)
     own_meta = pltpu.make_async_copy(smeta.at[me], got_meta.at[me], own_sem.at[1])
     own_meta.start()
 
@@ -196,18 +196,34 @@
         def _():
             pl.semaphore_wait(in_sem.at[s], 1)
 
-            def one(step, carry):
-                o = turned(own, lax.rem(step * 5, n_own), n_own)
-                send_rows(o, s)
-                send_meta(o, s)
-                return carry
-
-            lax.fori_loop(0, n_own, one, 0)
+    peers(send_rows, 1, hold, lambda s: early & (s > sub))
 
     @pl.when(early)
     def _():
         pl.semaphore_wait(late_sem, 1)
-        send_rows(0, 0)
+
+    turn = hold + lax.rem(me, n - hold)
+
+    def held(step, carry):
+        @pl.when(early & (step == turn))
+        def _():
+            send_rows(0, 0)
+
+        shift = lax.rem(step * 37, n)
+        o = turned(own, shift // n_sub, n_own)
+        s = lax.rem(sub + shift, n_sub)
+
+        @pl.when(o * n_sub + s != 0)
+        def _():
+            send_rows(o, s)
+
+        return carry
+
+    lax.fori_loop(hold, n, held, 0)
+    peers(send_meta, 1, n, lambda s: s >= 0)
+
+    @pl.when(early)
+    def _():
         send_meta(0, 0)
 
     part = pl.ds(0, n - 1)
@@ -238,6 +254,12 @@
         loads.append(pltpu.make_async_copy(got_rows.at[block], raw.at[block], in_sem.at[g]))
         stores.append(pltpu.make_async_copy(tidy.at[span], rows_out.at[span], out_sem.at[g]))
         loads[-1].start()
+    for g in range(n_own):
+        loads[g].wait()
+        tidy[pl.ds(g * n_sub * cap, n_sub * cap), :] = raw[
+            pl.ds(g * n_sub, n_sub)
+        ].reshape(n_sub * cap, depth)
+        stores[g].start()
     load_meta.wait()
     got = meta[...].astype(F32)
     got_counts, got_scores = got[:, 0, :], got[:, 1, :]
@@ -265,12 +287,6 @@
         .reshape(slots)
     )
     total_out[...] = jnp.sum(got_counts, axis=0, keepdims=True).astype(jnp.int32).reshape(n)
-    for g in range(n_own):
-        loads[g].wait()
-        tidy[pl.ds(g * n_sub * cap, n_sub * cap), :] = raw[
-            pl.ds(g * n_sub, n_sub)
-        ].reshape(n_sub * cap, depth)
-        stores[g].start()
     for store in stores:
         store.wait()
 

time: 72.5 us -> 55.9 us (0.77)
  the two profiles are of different devices: /device:TPU:640 before, /device:TPU:513 now
where the time goes in v3:
time: 55.9 us; the launch traced here: 55.7 us
  Pallas kernels  55.1 us (99%)
  between operations  0.64 us (1%)
    pallas_call x1, Pallas kernels, on_device(): pl.pallas_call(functools.partial(exchange, n_own, n_sub, cap), out_shape=...  52.2 us
    pallas_call x1, Pallas kernels, on_device(): pl.pallas_call(functools.partial(finish, n_own, n_sub, cap), out_shape=(j...  2.87 us

profile of v3, /device:TPU:513, one launch (start us, length us, event | category | flops | bytes accessed | tf_op | source)
XLA Modules:
  0.0 55.7 jit_solution(15228335091575718924)
XLA Ops:
  0.6 52.2 %shard_map.84 = (bf16[128,3,2,768]{3,2,1,0:T(2,128)(2,1)}, bf16[128,2,128]{2,1,0:T(2,128)(2,1)}) custom-call(bf16[512,768]{1,0:T(8,128)(2,1)} %emb_hbm.1, bf16[1000,768]{1,0:T(8,128)(2,1)} %table_hbm.1, s32[1,512]{1,0:T(1,128)} %bitcast.4, s32[1,1000]{1,0:T(1,128)} %bitcast.3, s32[1,512]{1,0:T(1,128)} %bitcast.5), custom_call_target="tpu_custom_call" | custom-call | tf_op jit(solution)/shard_map/pallas_call | solution.py:302
  52.9 2.9 %shard_map.85 = (bf16[768,768]{1,0:T(8,128)(2,1)}, bf16[768]{0:T(1024)(128)(2,1)}, s32[768]{0:T(1024)}, s32[128]{0:T(128)}) custom-call(bf16[128,3,2,768]{3,2,1,0:T(2,128)(2,1)} %get-tuple-element.6.got_rows, bf16[128,2,128]{2,1,0:T(2,128)(2,1)} %get-tuple-element.7.got_meta), custom_call_target="tpu_custom_call" | custom-call | tf_op jit(solution)/shard_map/pallas_call | solution.py:335

commit v4 on v3

--- a/solution.py
+++ b/solution.py
@@ -10,6 +10,7 @@
 MESH = pl.DeviceIdType.MESH
 BF = jnp.bfloat16
 F32 = jnp.float32
+MIDDLE = 1
 ROWS_AXES = ("groups", "owners", "sub")
 
 
@@ -155,7 +156,7 @@
 
     def peers(act, first, last, which):
         def one(step, carry):
-            shift = lax.rem(step * 37, n)
+            shift = lax.rem(step * 77, n)
             o = turned(own, shift // n_sub, n_own)
             s = lax.rem(sub + shift, n_sub)
 
@@ -190,13 +191,16 @@
     own_meta = pltpu.make_async_copy(smeta.at[me], got_meta.at[me], own_sem.at[1])
     own_meta.start()
 
-    for s in range(1, n_sub):
-
-        @pl.when(early & (s > sub))
-        def _():
-            pl.semaphore_wait(in_sem.at[s], 1)
-
-    peers(send_rows, 1, hold, lambda s: early & (s > sub))
+    for first, last in ((1, MIDDLE), (MIDDLE, n_sub)):
+        for s in range(first, last):
+
+            @pl.when(early & (s > sub))
+            def _(s=s):
+                pl.semaphore_wait(in_sem.at[s], 1)
+
+        @pl.when(early & (sub < last - 1))
+        def _(first=first, last=last):
+            peers(send_rows, 1, hold, lambda s: (s > sub) & (s >= first) & (s < last))
 
     @pl.when(early)
     def _():
@@ -209,7 +213,7 @@
         def _():
             send_rows(0, 0)
 
-        shift = lax.rem(step * 37, n)
+        shift = lax.rem(step * 77, n)
         o = turned(own, shift // n_sub, n_own)
         s = lax.rem(sub + shift, n_sub)
 
@@ -239,29 +243,19 @@
     n_own, n_sub, cap,
     got_rows, got_meta,
     rows_out, score_out, pos_out, total_out,
-    raw, meta, tidy, in_sem, out_sem, meta_sem,
+    tidy, out_sem,
 ):
     n = n_own * n_sub
     me = lax.axis_index("owners") * n_sub + lax.axis_index("sub")
     slots = n * cap
-    depth = raw.shape[-1]
-    load_meta = pltpu.make_async_copy(got_meta, meta, meta_sem)
-    load_meta.start()
-    loads, stores = [], []
+    depth = got_rows.shape[-1]
+    stores = []
     for g in range(n_own):
-        block = pl.ds(g * n_sub, n_sub)
         span = pl.ds(g * n_sub * cap, n_sub * cap)
-        loads.append(pltpu.make_async_copy(got_rows.at[block], raw.at[block], in_sem.at[g]))
+        tidy[span, :] = got_rows[pl.ds(g * n_sub, n_sub)].reshape(n_sub * cap, depth)
         stores.append(pltpu.make_async_copy(tidy.at[span], rows_out.at[span], out_sem.at[g]))
-        loads[-1].start()
-    for g in range(n_own):
-        loads[g].wait()
-        tidy[pl.ds(g * n_sub * cap, n_sub * cap), :] = raw[
-            pl.ds(g * n_sub, n_sub)
-        ].reshape(n_sub * cap, depth)
-        stores[g].start()
-    load_meta.wait()
-    got = meta[...].astype(F32)
+        stores[-1].start()
+    got = got_meta[...].astype(F32)
     got_counts, got_scores = got[:, 0, :], got[:, 1, :]
     source = iota((n, slots), 1) // cap
     step_in = lax.rem(iota((1, slots), 1), cap)
@@ -302,11 +296,11 @@
     got_rows, got_meta = pl.pallas_call(
         functools.partial(exchange, n_own, n_sub, cap),
         out_shape=(
-            jax.ShapeDtypeStruct((n, cap // 2, 2, depth), BF),
-            jax.ShapeDtypeStruct((n, 2, 128), BF),
+            pltpu.VMEM((n, cap // 2, 2, depth), BF),
+            pltpu.VMEM((n, 2, 128), BF),
         ),
         in_specs=[hbm] * 5,
-        out_specs=(hbm, hbm),
+        out_specs=(vmem, vmem),
         scratch_shapes=[
             pltpu.VMEM((rows, depth), BF),
             pltpu.VMEM((classes, depth), BF),
@@ -340,17 +334,16 @@
             jax.ShapeDtypeStruct((slots,), jnp.int32),
             jax.ShapeDtypeStruct((n,), jnp.int32),
         ),
-        in_specs=[hbm, hbm],
+        in_specs=[vmem, vmem],
         out_specs=(hbm, vmem, vmem, vmem),
         scratch_shapes=[
-            pltpu.VMEM((n, cap // 2, 2, depth), BF),
-            pltpu.VMEM((n, 2, 128), BF),
             pltpu.VMEM((slots, depth), BF),
             pltpu.SemaphoreType.DMA((n_own,)),
-            pltpu.SemaphoreType.DMA((n_own,)),
-            pltpu.SemaphoreType.DMA,
         ],
-    )(got_rows, got_meta)
+    )(
+        pltpu.with_memory_space_constraint(got_rows, pltpu.VMEM),
+        pltpu.with_memory_space_constraint(got_meta, pltpu.VMEM),
+    )
 
 
 def solution(mesh):

time: 55.9 us -> 54 us (0.966)
  Pallas kernels: 55.1 us -> 53.3 us
    pallas_call x1, Pallas kernels: 52.2 us -> 51.1 us  [on_device(): pl.pallas_call(functools.partial(exchange, n_own, n_sub, cap), out_shape=...]
    pallas_call x1, Pallas kernels: 2.87 us -> 2.13 us  [on_device(): pl.pallas_call(functools.partial(finish, n_own, n_sub, cap), out_shape=(j...]
where the time goes in v4:
time: 54 us; the launch traced here: 53.9 us
  Pallas kernels  53.3 us (99%)
  between operations  0.64 us (1%)
    pallas_call x1, Pallas kernels, on_device(): pl.pallas_call(functools.partial(exchange, n_own, n_sub, cap), out_shape=...  51.1 us
    pallas_call x1, Pallas kernels, on_device(): pl.pallas_call(functools.partial(finish, n_own, n_sub, cap), out_shape=(j...  2.13 us

profile of v4, /device:TPU:513, one launch (start us, length us, event | category | flops | bytes accessed | tf_op | source)
XLA Modules:
  0.0 53.9 jit_solution(1994732817331371369)
XLA Ops:
  0.6 51.1 %shard_map.84 = (bf16[128,3,2,768]{3,2,1,0:T(2,128)(2,1)S(1)}, bf16[128,2,128]{2,1,0:T(2,128)(2,1)S(1)}) custom-call(bf16[512,768]{1,0:T(8,128)(2,1)} %emb_hbm.1, bf16[1000,768]{1,0:T(8,128)(2,1)} %table_hbm.1, s32[1,512]{1,0:T(1,128)} %bitcast.4, s32[1,1000]{1,0:T(1,128)} %bitcast.3, s32[1,512]{1,0:T(1,128)} %bitcast.5), custom_call_target="tpu_custom_call" | custom-call | tf_op jit(solution)/shard_map/pallas_call | solution.py:296
  51.8 2.1 %shard_map.85 = (bf16[768,768]{1,0:T(8,128)(2,1)}, bf16[768]{0:T(1024)(128)(2,1)}, s32[768]{0:T(1024)}, s32[128]{0:T(128)}) custom-call(bf16[128,3,2,768]{3,2,1,0:T(2,128)(2,1)S(1)} %get-tuple-element.6.got_rows, bf16[128,2,128]{2,1,0:T(2,128)(2,1)S(1)} %get-tuple-element.7.got_meta), custom_call_target="tpu_custom_call" | custom-call | tf_op jit(solution)/shard_map/pallas_call | solution.py:329

commit v5 on v4

--- a/solution.py
+++ b/solution.py
@@ -10,7 +10,6 @@
 MESH = pl.DeviceIdType.MESH
 BF = jnp.bfloat16
 F32 = jnp.float32
-MIDDLE = 1
 ROWS_AXES = ("groups", "owners", "sub")
 
 
@@ -34,8 +33,8 @@
 def exchange(
     n_own, n_sub, cap,
     emb_hbm, table_hbm, near_hbm, keep_hbm, dest_hbm,
-    got_rows, got_meta,
-    emb, table, near, keep, dest, sbuf, smeta,
+    tidy, got_meta,
+    emb, table, near, keep, dest, sbuf, got_rows, smeta,
     load_sem, own_sem, row_send, row_recv, meta_send, meta_recv, in_sem, late_sem,
 ):
     own, sub = lax.axis_index("owners"), lax.axis_index("sub")
@@ -45,7 +44,11 @@
     classes = table.shape[0]
 
     barrier = pltpu.get_barrier_semaphore()
-    late = me == 0
+    has_late = lax.axis_index("groups") == 0
+    late = has_late & (me == 0)
+
+    def apart(o, s):
+        return has_late & (o == 0) & (s == 0)
     hold = n * 5 // 8
     early = jnp.logical_not(late)
 
@@ -72,7 +75,7 @@
     def greet_row(step, carry):
         o = turned(own, step, n_own)
 
-        @pl.when(early & (o * n_sub + sub != 0))
+        @pl.when(early & jnp.logical_not(apart(o, sub)))
         def _():
             tell(barrier, o, sub)
 
@@ -99,16 +102,20 @@
     packed = dot(place, emb[...], ((1,), (0,))).astype(BF)
     sbuf[...] = packed.reshape(n, cap // 2, 2, depth)
 
-    @pl.when(early & (sub == 0))
+    @pl.when(early & (sub == 0) & has_late)
     def _():
         pl.semaphore_wait(barrier, n_own - 2)
         tell(barrier, 0, 0)
 
+    @pl.when((sub == 0) & jnp.logical_not(has_late))
+    def _():
+        pl.semaphore_wait(barrier, n_own - 1)
+
     @pl.when(sub != 0)
     def _():
         pl.semaphore_wait(barrier, n_own - 1 + sub)
 
-    @pl.when((own == 0) & (sub != 0))
+    @pl.when(has_late & (own == 0) & (sub != 0))
     def _():
         tell(barrier, 0, 0)
 
@@ -121,11 +128,11 @@
         def _():
             tell(barrier, own, s)
 
-        @pl.when((own == 1) & (sub == 0) & (s > 0))
+        @pl.when(has_late & (own == 1) & (sub == 0) & (s > 0))
         def _():
             tell(barrier, 0, s)
 
-        @pl.when((s < sub) & (own * n_sub + s != 0))
+        @pl.when((s < sub) & jnp.logical_not(apart(own, s)))
         def _():
             tell(in_sem.at[sub], own, s)
 
@@ -144,7 +151,7 @@
 
     def send_rows(o, s):
         pltpu.make_async_remote_copy(
-            sbuf.at[o * n_sub + s], got_rows.at[me], row_send, row_recv,
+            sbuf.at[o * n_sub + s], got_rows.at[me], row_send, row_recv.at[own],
             device_id={"owners": o, "sub": s}, device_id_type=MESH,
         ).start()
 
@@ -160,7 +167,7 @@
             o = turned(own, shift // n_sub, n_own)
             s = lax.rem(sub + shift, n_sub)
 
-            @pl.when(which(s) & (o * n_sub + s != 0))
+            @pl.when(which(s) & jnp.logical_not(apart(o, s)))
             def _():
                 act(o, s)
 
@@ -169,8 +176,7 @@
         lax.fori_loop(first, last, one, 0)
 
     peers(send_rows, 1, hold, lambda s: late | (s <= sub))
-    own_rows = pltpu.make_async_copy(sbuf.at[me], got_rows.at[me], own_sem.at[0])
-    own_rows.start()
+    pltpu.make_async_copy(sbuf.at[me], got_rows.at[me], row_recv.at[own]).start()
 
     loads[4].wait()
     emb_f = emb[...].astype(F32)
@@ -188,28 +194,27 @@
     meta = jnp.stack([jnp.broadcast_to(counts, (n, n)), scores], axis=1)
     smeta[...] = meta.astype(BF)
 
-    own_meta = pltpu.make_async_copy(smeta.at[me], got_meta.at[me], own_sem.at[1])
+    own_meta = pltpu.make_async_copy(smeta.at[me], got_meta.at[me], own_sem)
     own_meta.start()
 
-    for first, last in ((1, MIDDLE), (MIDDLE, n_sub)):
-        for s in range(first, last):
-
-            @pl.when(early & (s > sub))
-            def _(s=s):
-                pl.semaphore_wait(in_sem.at[s], 1)
-
-        @pl.when(early & (sub < last - 1))
-        def _(first=first, last=last):
-            peers(send_rows, 1, hold, lambda s: (s > sub) & (s >= first) & (s < last))
-
-    @pl.when(early)
+    for s in range(1, n_sub):
+
+        @pl.when(early & (s > sub))
+        def _(s=s):
+            pl.semaphore_wait(in_sem.at[s], 1)
+
+    @pl.when(early & (sub < n_sub - 1))
+    def _():
+        peers(send_rows, 1, hold, lambda s: s > sub)
+
+    @pl.when(early & has_late)
     def _():
         pl.semaphore_wait(late_sem, 1)
 
     turn = hold + lax.rem(me, n - hold)
 
     def held(step, carry):
-        @pl.when(early & (step == turn))
+        @pl.when(early & has_late & (step == turn))
         def _():
             send_rows(0, 0)
 
@@ -217,7 +222,7 @@
         o = turned(own, shift // n_sub, n_own)
         s = lax.rem(sub + shift, n_sub)
 
-        @pl.when(o * n_sub + s != 0)
+        @pl.when(jnp.logical_not(apart(o, s)))
         def _():
             send_rows(o, s)
 
@@ -226,35 +231,34 @@
     lax.fori_loop(hold, n, held, 0)
     peers(send_meta, 1, n, lambda s: s >= 0)
 
-    @pl.when(early)
+    @pl.when(early & has_late)
     def _():
         send_meta(0, 0)
 
     part = pl.ds(0, n - 1)
     pltpu.make_async_copy(sbuf.at[part], got_rows.at[part], row_send).wait()
     pltpu.make_async_copy(smeta.at[part], got_meta.at[part], meta_send).wait()
-    own_rows.wait()
     own_meta.wait()
-    pltpu.make_async_copy(sbuf.at[part], got_rows.at[part], row_recv).wait()
+    for g in (*range(1, n_own), 0):
+        block = pl.ds(g * n_sub, n_sub)
+        pltpu.make_async_copy(sbuf.at[block], got_rows.at[block], row_recv.at[g]).wait()
+        tidy[pl.ds(g * n_sub * cap, n_sub * cap), :] = got_rows[block].reshape(
+            n_sub * cap, depth
+        )
     pltpu.make_async_copy(smeta.at[part], got_meta.at[part], meta_recv).wait()
 
 
 def finish(
     n_own, n_sub, cap,
-    got_rows, got_meta,
+    tidy, got_meta,
     rows_out, score_out, pos_out, total_out,
-    tidy, out_sem,
+    out_sem,
 ):
     n = n_own * n_sub
     me = lax.axis_index("owners") * n_sub + lax.axis_index("sub")
     slots = n * cap
-    depth = got_rows.shape[-1]
-    stores = []
-    for g in range(n_own):
-        span = pl.ds(g * n_sub * cap, n_sub * cap)
-        tidy[span, :] = got_rows[pl.ds(g * n_sub, n_sub)].reshape(n_sub * cap, depth)
-        stores.append(pltpu.make_async_copy(tidy.at[span], rows_out.at[span], out_sem.at[g]))
-        stores[-1].start()
+    store = pltpu.make_async_copy(tidy, rows_out, out_sem)
+    store.start()
     got = got_meta[...].astype(F32)
     got_counts, got_scores = got[:, 0, :], got[:, 1, :]
     source = iota((n, slots), 1) // cap
@@ -281,8 +285,7 @@
         .reshape(slots)
     )
     total_out[...] = jnp.sum(got_counts, axis=0, keepdims=True).astype(jnp.int32).reshape(n)
-    for store in stores:
-        store.wait()
+    store.wait()
 
 
 def on_device(n_own, n_sub, embeddings, class_table, nearest, keep_class, destination):
@@ -293,10 +296,10 @@
     slots = n * cap
     vmem = pl.BlockSpec(memory_space=pltpu.VMEM)
     hbm = pl.BlockSpec(memory_space=pl.ANY)
-    got_rows, got_meta = pl.pallas_call(
+    tidy, got_meta = pl.pallas_call(
         functools.partial(exchange, n_own, n_sub, cap),
         out_shape=(
-            pltpu.VMEM((n, cap // 2, 2, depth), BF),
+            pltpu.VMEM((slots, depth), BF),
             pltpu.VMEM((n, 2, 128), BF),
         ),
         in_specs=[hbm] * 5,
@@ -308,11 +311,12 @@
             pltpu.VMEM((1, classes), jnp.int32),
             pltpu.VMEM((1, rows), jnp.int32),
             pltpu.VMEM((n, cap // 2, 2, depth), BF),
+            pltpu.VMEM((n, cap // 2, 2, depth), BF),
             pltpu.VMEM((n, 2, 128), BF),
             pltpu.SemaphoreType.DMA((5,)),
-            pltpu.SemaphoreType.DMA((2,)),
-            pltpu.SemaphoreType.DMA,
-            pltpu.SemaphoreType.DMA,
+            pltpu.SemaphoreType.DMA,
+            pltpu.SemaphoreType.DMA,
+            pltpu.SemaphoreType.DMA((n_own,)),
             pltpu.SemaphoreType.DMA,
             pltpu.SemaphoreType.DMA,
             pltpu.SemaphoreType.REGULAR((n_sub,)),
@@ -337,11 +341,10 @@
         in_specs=[vmem, vmem],
         out_specs=(hbm, vmem, vmem, vmem),
         scratch_shapes=[
-            pltpu.VMEM((slots, depth), BF),
-            pltpu.SemaphoreType.DMA((n_own,)),
+            pltpu.SemaphoreType.DMA,
         ],
     )(
-        pltpu.with_memory_space_constraint(got_rows, pltpu.VMEM),
+        pltpu.with_memory_space_constraint(tidy, pltpu.VMEM),
         pltpu.with_memory_space_constraint(got_meta, pltpu.VMEM),
     )
 

time: 54 us -> 53.3 us (0.987)
  Pallas kernels: 53.3 us -> 52.6 us
where the time goes in v5:
time: 53.3 us; the launch traced here: 53.2 us
  Pallas kernels  52.6 us (99%)
  between operations  0.64 us (1%)
    pallas_call x1, Pallas kernels, on_device(): pl.pallas_call(functools.partial(exchange, n_own, n_sub, cap), out_shape=...  50.9 us
    pallas_call x1, Pallas kernels, on_device(): pl.pallas_call(functools.partial(finish, n_own, n_sub, cap), out_shape=(j...  1.62 us

profile of v5, /device:TPU:513, one launch (start us, length us, event | category | flops | bytes accessed | tf_op | source)
XLA Modules:
  0.0 53.2 jit_solution(11871615877050381630)
XLA Ops:
  0.6 50.9 %shard_map.84 = (bf16[768,768]{1,0:T(8,128)(2,1)S(1)}, bf16[128,2,128]{2,1,0:T(2,128)(2,1)S(1)}) custom-call(bf16[512,768]{1,0:T(8,128)(2,1)} %emb_hbm.1, bf16[1000,768]{1,0:T(8,128)(2,1)} %table_hbm.1, s32[1,512]{1,0:T(1,128)} %bitcast.4, s32[1,1000]{1,0:T(1,128)} %bitcast.3, s32[1,512]{1,0:T(1,128)} %bitcast.5), custom_call_target="tpu_custom_call" | custom-call | tf_op jit(solution)/shard_map/pallas_call | solution.py:299
  51.6 1.6 %shard_map.85 = (bf16[768,768]{1,0:T(8,128)(2,1)}, bf16[768]{0:T(1024)(128)(2,1)}, s32[768]{0:T(1024)}, s32[128]{0:T(128)}) custom-call(bf16[768,768]{1,0:T(8,128)(2,1)S(1)} %get-tuple-element.6.tidy, bf16[128,2,128]{2,1,0:T(2,128)(2,1)S(1)} %get-tuple-element.7.got_meta), custom_call_target="tpu_custom_call" | custom-call | tf_op jit(solution)/shard_map/pallas_call | solution.py:333

commit v6 on v5

--- a/solution.py
+++ b/solution.py
@@ -49,7 +49,7 @@
 
     def apart(o, s):
         return has_late & (o == 0) & (s == 0)
-    hold = n * 5 // 8
+    hold = n * 19 // 32
     early = jnp.logical_not(late)
 
     def tell(sem, o, s):
@@ -83,6 +83,19 @@
 
     lax.fori_loop(1, n_own, greet_row, 0)
 
+    @pl.when(late)
+    def _():
+        pl.semaphore_wait(barrier, n_own - 1 + n_sub - 1)
+
+    def tell_late(i, carry):
+        @pl.when(late)
+        def _():
+            tell(late_sem, i // n_sub, lax.rem(i, n_sub))
+
+        return carry
+
+    lax.fori_loop(1, n, tell_late, 0)
+
     loads[0].wait()
     loads[1].wait()
     loads[2].wait()
@@ -119,10 +132,6 @@
     def _():
         tell(barrier, 0, 0)
 
-    @pl.when(late)
-    def _():
-        pl.semaphore_wait(barrier, n_own - 1 + n_sub - 1)
-
     def tell_column(s, carry):
         @pl.when(early & (s > sub))
         def _():
@@ -139,15 +148,6 @@
         return carry
 
     lax.fori_loop(0, n_sub, tell_column, 0)
-
-    def tell_late(i, carry):
-        @pl.when(late)
-        def _():
-            tell(late_sem, i // n_sub, lax.rem(i, n_sub))
-
-        return carry
-
-    lax.fori_loop(1, n, tell_late, 0)
 
     def send_rows(o, s):
         pltpu.make_async_remote_copy(

time: 53.3 us -> 52.9 us (level)
  no operation moved by 1% of the time
where the time goes in v6:
time: 52.9 us; the launch traced here: 52.8 us
  Pallas kernels  52.2 us (99%)
  between operations  0.64 us (1%)
    pallas_call x1, Pallas kernels, on_device(): pl.pallas_call(functools.partial(exchange, n_own, n_sub, cap), out_shape=...  50.6 us
    pallas_call x1, Pallas kernels, on_device(): pl.pallas_call(functools.partial(finish, n_own, n_sub, cap), out_shape=(j...  1.62 us

profile of v6, /device:TPU:513, one launch (start us, length us, event | category | flops | bytes accessed | tf_op | source)
XLA Modules:
  0.0 52.8 jit_solution(2134618891889815384)
XLA Ops:
  0.6 50.6 %shard_map.84 = (bf16[768,768]{1,0:T(8,128)(2,1)S(1)}, bf16[128,2,128]{2,1,0:T(2,128)(2,1)S(1)}) custom-call(bf16[512,768]{1,0:T(8,128)(2,1)} %emb_hbm.1, bf16[1000,768]{1,0:T(8,128)(2,1)} %table_hbm.1, s32[1,512]{1,0:T(1,128)} %bitcast.4, s32[1,1000]{1,0:T(1,128)} %bitcast.3, s32[1,512]{1,0:T(1,128)} %bitcast.5), custom_call_target="tpu_custom_call" | custom-call | tf_op jit(solution)/shard_map/pallas_call | solution.py:299
  51.2 1.6 %shard_map.85 = (bf16[768,768]{1,0:T(8,128)(2,1)}, bf16[768]{0:T(1024)(128)(2,1)}, s32[768]{0:T(1024)}, s32[128]{0:T(128)}) custom-call(bf16[768,768]{1,0:T(8,128)(2,1)S(1)} %get-tuple-element.6.tidy, bf16[128,2,128]{2,1,0:T(2,128)(2,1)S(1)} %get-tuple-element.7.got_meta), custom_call_target="tpu_custom_call" | custom-call | tf_op jit(solution)/shard_map/pallas_call | solution.py:333
